TPU v7x, 32 devices: a whole 2x2x4 slice. The times are simulated.
32 devices in a mesh: seq: 16 (over z, y, x), head: 2 (over core).
Axes of the slice: x: 2, y: 2, z: 4, core: 2. Of those that a mesh axis runs over, the one named last changes fastest.
Arguments:
- hidden: bfloat16 [8192, 8192], P('seq', 'head'), may hold values from -6 to 6
- key_weight: bfloat16 [8192, 1024], P('head'), may hold values from -0.0625 to 0.0625
- value_weight: bfloat16 [8192, 1024], P('head'), may hold values from -0.0625 to 0.0625
- key_bias: float32 [1024], P('head'), may hold values from -5 to 5
- value_bias: float32 [1024], P('head'), may hold values from -5 to 5
- request_tokens: int32 [16], replicated, may hold values from 1 to 1024, 8192 in all
- request_context: int32 [16], replicated, may hold values from 0 to 4095
- page_owner: int32 [1024], replicated, may hold values from 0 to 15, as said below
- page_slot: int32 [1024], replicated, may hold values from 0 to 78
- key_cache: bfloat16 [1264, 8, 1024], P('seq', None, 'head'), may hold values from -1 to 1
- value_cache: bfloat16 [1264, 8, 1024], P('seq', None, 'head'), may hold values from -1 to 1
- stored_key_scales: bfloat16 [1264, 8], P('seq', 'head'), may hold values from 0.5 to 8
- value_scales: bfloat16 [1264, 8], P('seq', 'head'), may hold values from 0.5 to 8
Outputs:
- new_key_cache: bfloat16 [1264, 8, 1024], P('seq', None, 'head')
- new_value_cache: bfloat16 [1264, 8, 1024], P('seq', None, 'head')
- new_key_scales: bfloat16 [1264, 8], P('seq', 'head')
- new_value_scales: bfloat16 [1264, 8], P('seq', 'head')
Inputs may be any that keep to these rules, and one draw needn't show every extreme that they name: No two pages name the same (page_owner, page_slot) pair. Each index of seq owns at most 79 pages of the block, and one owns exactly 79 in every draw. The 64 pages of one index of seq (pages i * 64 to (i + 1) * 64 - 1) go at most 5 to one owner, and some index sends exactly 5 to one owner in every draw.
All inputs are finite; a program needn't handle non-finite values.
Results may differ from a plain program's by a relative error of at most 0.0065.
Values may be sent and summed in bfloat16 or wider, within the bound.
A program may use at most 128 MiB of HBM per device.

v0:
```python
import jax
import jax.numpy as jnp
from jax import lax
from jax.sharding import PartitionSpec as P

rope_base = 1000000.0
eps = 1e-06


def positions_of(request_tokens, request_context, token_ids):
    ends = jnp.cumsum(request_tokens)
    starts = ends - request_tokens
    inside = (token_ids[:, None] >= starts[None, :]) & (token_ids[:, None] < ends[None, :])
    offset = jnp.sum(jnp.where(inside, (request_context - starts)[None, :], 0), axis=1)
    return offset + token_ids


def rotate(values, positions, head_dim):
    half = head_dim // 2
    freqs = jnp.exp(
        -jnp.log(jnp.float32(rope_base)) * (2.0 * jnp.arange(half).astype(jnp.float32) / head_dim)
    )
    angle = positions.astype(jnp.float32)[:, None] * freqs[None, :]
    cosine = jnp.cos(angle)[:, None, :]
    sine = jnp.sin(angle)[:, None, :]
    first = values[..., :half]
    second = values[..., half:]
    return jnp.concatenate(
        [first * cosine - second * sine, second * cosine + first * sine], axis=-1
    )


def normalize(pages):
    largest = jnp.max(jnp.abs(pages.astype(jnp.float32)), axis=(1, 3))
    scale = (largest + eps).astype(jnp.bfloat16)
    codes = (pages.astype(jnp.float32) / scale.astype(jnp.float32)[:, None, :, None]).astype(
        jnp.bfloat16
    )
    return (codes, scale)


def shards(
    hidden,
    key_weight,
    value_weight,
    key_bias,
    value_bias,
    request_tokens,
    request_context,
    page_owner,
    page_slot,
    key_cache,
    value_cache,
    stored_key_scales,
    value_scales,
):
    tok_rows = hidden.shape[0]
    slots_here, page_len, columns = key_cache.shape
    local_head_count = stored_key_scales.shape[1]
    head_dim = columns // local_head_count
    pages_here = tok_rows // page_len
    sequence_count = lax.axis_size("seq")
    seq_index = lax.axis_index("seq")
    capacity = (pages_here + sequence_count - 1) // sequence_count + 1
    key_part = jnp.dot(hidden, key_weight, preferred_element_type=jnp.float32)
    value_part = jnp.dot(hidden, value_weight, preferred_element_type=jnp.float32)
    key_proj, value_proj = (
        lax.psum_scatter(key_part, "head", scatter_dimension=1, tiled=True),
        lax.psum_scatter(value_part, "head", scatter_dimension=1, tiled=True),
    )
    token_ids = seq_index * tok_rows + jnp.arange(tok_rows)
    positions = positions_of(request_tokens, request_context, token_ids)
    key_raw = (key_proj + key_bias).reshape(tok_rows, local_head_count, head_dim)
    keys = rotate(key_raw, positions, head_dim).astype(jnp.bfloat16)
    values = (value_proj + value_bias).astype(jnp.bfloat16)
    total_pages = page_owner.shape[0]
    page_ids = jnp.arange(total_pages)
    senders = page_ids // pages_here
    owner_blocks = page_owner.reshape(sequence_count, pages_here)
    within = jnp.arange(pages_here)
    before = (owner_blocks[:, :, None] == owner_blocks[:, None, :]) & (
        within[None, None, :] < within[None, :, None]
    )
    rank = jnp.sum(before.astype(jnp.int32), axis=2).reshape(total_pages)
    lane = senders * capacity + rank
    own_owner = lax.dynamic_slice_in_dim(page_owner, seq_index * pages_here, pages_here, 0)
    own_rank = lax.dynamic_slice_in_dim(rank, seq_index * pages_here, pages_here, 0)
    destination = own_owner * capacity + own_rank
    buffer_rows = sequence_count * capacity
    placing = (jnp.arange(buffer_rows)[:, None] == destination[None, :]).astype(jnp.bfloat16)

    def pack(array):
        flat = array.reshape(pages_here, -1)
        placed = jnp.dot(placing, flat, preferred_element_type=jnp.float32).astype(array.dtype)
        return placed.reshape((sequence_count, capacity) + array.shape[1:])

    raw = (
        pack(keys.reshape(pages_here, page_len, columns)),
        pack(values.reshape(pages_here, page_len, columns)),
    )
    key_part = lax.all_to_all(raw[0], "seq", split_axis=0, concat_axis=0, tiled=True)
    value_part = lax.all_to_all(raw[1], "seq", split_axis=0, concat_axis=0, tiled=True)
    element_list = key_part.shape[1]
    shaped = (sequence_count * element_list, page_len, local_head_count, head_dim)
    key_codes, key_page_scale = normalize(key_part.reshape(shaped))
    value_codes, value_scale = normalize(value_part.reshape(shaped))
    got_keys = key_codes.reshape(sequence_count, element_list, page_len, columns)
    got_values = value_codes.reshape(sequence_count, element_list, page_len, columns)
    received_key_scale = key_page_scale.reshape(sequence_count, element_list, local_head_count)
    got_vscale = value_scale.reshape(sequence_count, element_list, local_head_count)
    mine = page_owner == seq_index
    slot_hits = ((page_slot[:, None] == jnp.arange(slots_here)[None, :]) & mine[:, None]).astype(
        jnp.float32
    )
    lane_hits = (lane[:, None] == jnp.arange(buffer_rows)[None, :]).astype(jnp.float32)
    chooser = jnp.dot(slot_hits.T, lane_hits, preferred_element_type=jnp.float32).astype(
        jnp.bfloat16
    )
    written = jnp.sum(slot_hits, axis=0) > 0.5

    def unpack_entries(received, old):
        flat = received.reshape(buffer_rows, -1)
        placed = (
            jnp.dot(chooser, flat, preferred_element_type=jnp.float32)
            .astype(old.dtype)
            .reshape(old.shape)
        )
        keep = written.reshape((slots_here,) + (1,) * (old.ndim - 1))
        return jnp.where(keep, placed, old)

    return (
        unpack_entries(got_keys, key_cache),
        unpack_entries(got_values, value_cache),
        unpack_entries(received_key_scale, stored_key_scales),
        unpack_entries(got_vscale, value_scales),
    )


def solution(mesh):
    placed = (
        P("seq", "head"),
        P("head", None),
        P("head", None),
        P("head"),
        P("head"),
        P(),
        P(),
        P(),
        P(),
        P("seq", None, "head"),
        P("seq", None, "head"),
        P("seq", "head"),
        P("seq", "head"),
    )
    return jax.shard_map(
        shards,
        mesh=mesh,
        in_specs=placed,
        out_specs=(
            P("seq", None, "head"),
            P("seq", None, "head"),
            P("seq", "head"),
            P("seq", "head"),
        ),
        check_vma=False,
    )
```

profile of v0, /device:TPU:0, one launch (start us, length us, event | category | flops | bytes accessed | tf_op | source)
XLA Modules:
  0.0 97.9 jit_solution(11579516915367683486)
XLA Ops:
  7.2 0.0 reduce-scatter.3.cloned.1.call-start
  7.2 10.4 %fusion.19 = f32[512,1024]{1,0:T(8,128)} fusion(bf16[512,4096]{1,0:T(8,128)(2,1)} %param.13, bf16[4096,1024]{1,0:T(8,128)(2,1)} %param.14), kind=kOutput, calls=%fused_computation.57 | convolution fusion | flops 4294967296 | bytes 14680064 | tf_op jit(solution)/shard_map/dot_general | solution.py:65
  17.7 0.0 reduce-scatter.3.cloned.1.call-update
  17.7 0.0 reduce-scatter.5.cloned.1.call-start
  17.7 10.5 %fusion.20 = f32[512,1024]{1,0:T(8,128)} fusion(bf16[512,4096]{1,0:T(8,128)(2,1)} %param.13, bf16[4096,1024]{1,0:T(8,128)(2,1)} %param.15), kind=kOutput, calls=%fused_computation.58 | convolution fusion | flops 4294967296 | bytes 14680064 | tf_op jit(solution)/shard_map/dot_general | solution.py:66
  28.2 0.0 reduce-scatter.5.cloned.1.call-update
  28.3 0.6 copy-done.8
  28.9 0.1 copy.19
  29.0 0.1 reduce.4
  29.1 0.0 copy-done.4
  29.1 0.1 eq.65
  29.2 0.5 convert_reduce_fusion
  29.7 0.1 reshape.189
  29.8 0.1 dynamic-slice_add_fusion
  29.9 0.1 select_reduce_fusion
  30.0 1.0 %multiply_cosine_fusion = (f32[512,64]{1,0:T(8,128)S(1)}, f32[512,64]{1,0:T(8,128)S(1)}) fusion(f32[64]{0:T(128)S(1)} %multiply_exponential_fusion, f32[512]{0:T(512)S(1)} %add_convert_fusion.6), kind=kLoop, calls=%fused_computation.23 | loop fusion | flops 32768 | bytes 264448 | tf_op jit(solution)/shard_map/cos | solution.py:24
  31.0 0.0 reduce-scatter.3.cloned.1.call-done
  31.0 1.4 %broadcast_add_fusion = f32[512,512]{1,0:T(8,128)S(1)} fusion(f32[512,512]{1,0:T(8,128)} %reduce-scatter.3.cloned.1.call-done, f32[512]{0:T(512)S(1)} %copy-done.6), kind=kLoop, calls=%fused_computation.19 | loop fusion | flops 262144 | bytes 2099200 | tf_op jit(solution)/shard_map/add | solution.py:73
  32.4 0.4 reshape.190
  32.8 0.8 subtract_convert_fusion
  33.6 0.7 pad_maximum_fusion
  34.3 0.4 convert_element_type.114
  34.7 0.3 convolution_convert_fusion.1
  35.0 0.0 copy-start.5
  35.0 0.0 copy-start.7
  35.0 1.1 %copy.20 = bf16[10,8,8,512]{3,2,1,0:T(8,128)(2,1)} copy(bf16[10,8,8,512]{3,1,2,0:T(8,128)(2,1)S(1)} %bitcast.34) | data formatting | bytes 1310720
  36.1 8.3 %all-to-all-start = ((bf16[16,5,8,512]{3,2,1,0:T(8,128)(2,1)}), bf16[16,5,8,512]{3,2,1,0:T(8,128)(2,1)S(1)}, u32[]{:S(2)}, u32[]{:S(2)}) async-start(bf16[16,5,8,512]{3,2,1,0:T(8,128)(2,1)} %bitcast.3), calls=%async_computation.1 | async-start | bytes 1310720 | tf_op jit(solution)/shard_map/all_to_all | solution.py:101
  44.5 0.2 convert_reduce_fusion.1
  44.6 0.0 reduce-scatter.5.cloned.1.call-done
  44.6 1.3 %add_convert_fusion = bf16[512,512]{1,0:T(8,128)(2,1)S(1)} fusion(f32[512,512]{1,0:T(8,128)} %reduce-scatter.5.cloned.1.call-done, f32[512]{0:T(512)S(1)} %copy-done.7), kind=kLoop, calls=%fused_computation.13 | loop fusion | flops 524288 | bytes 1574912 | tf_op jit(solution)/shard_map/convert_element_type | solution.py:75
  46.0 0.2 reshape_reshape.2
  46.2 0.3 convolution_convert_fusion
  46.6 1.1 %copy.23 = bf16[10,8,8,512]{3,2,1,0:T(8,128)(2,1)} copy(bf16[10,8,8,512]{3,1,2,0:T(8,128)(2,1)S(1)} %bitcast.33) | data formatting | bytes 1310720
  47.7 14.1 %all-to-all-done = bf16[16,5,8,512]{3,2,1,0:T(8,128)(2,1)S(1)} async-done(((bf16[16,5,8,512]{3,2,1,0:T(8,128)(2,1)}), bf16[16,5,8,512]{3,2,1,0:T(8,128)(2,1)S(1)}, u32[]{:S(2)}, u32[]{:S(2)}) %all-to-all-start) | async-done | bytes 655392 | tf_op jit(solution)/shard_map/all_to_all | solution.py:101
  61.8 4.5 %all-to-all-start.1 = ((bf16[16,5,8,512]{3,2,1,0:T(8,128)(2,1)}), bf16[16,5,8,512]{3,2,1,0:T(8,128)(2,1)S(1)}, u32[]{:S(2)}, u32[]{:S(2)}) async-start(bf16[16,5,8,512]{3,2,1,0:T(8,128)(2,1)} %bitcast.12), calls=%async_computation.3 | async-start | bytes 1310720 | tf_op jit(solution)/shard_map/all_to_all | solution.py:102
  66.3 0.4 convolution_convert_fusion.4
  66.7 0.4 abs_reduce_fusion.1
  67.1 0.1 reduce_max.24
  67.2 0.2 reduce_max.25
  67.4 0.2 div.34
  67.6 1.6 %div.35 = f32[80,4096]{1,0:T(8,128)} reshape(f32[80,8,4,128]{3,2,1,0:T(4,128)S(1)} %div.34) | data formatting | bytes 2621440 | tf_op jit(solution)/shard_map/div | solution.py:36
  69.2 0.2 copy.21
  69.5 1.1 %copy-done.1 = f32[80,4096]{1,0:T(8,128)S(1)} copy-done((f32[80,4096]{1,0:T(8,128)S(1)}, f32[80,4096]{1,0:T(8,128)}, u32[]{:S(2)}) %copy-start.1) | copy-done | bytes 1310744
  70.5 0.3 convolution_convert_fusion.3
  70.9 0.0 copy-start.9
  70.9 0.0 copy-start.10
  70.9 0.2 copy.22
  71.1 11.6 %all-to-all-done.1 = bf16[16,5,8,512]{3,2,1,0:T(8,128)(2,1)S(1)} async-done(((bf16[16,5,8,512]{3,2,1,0:T(8,128)(2,1)}), bf16[16,5,8,512]{3,2,1,0:T(8,128)(2,1)S(1)}, u32[]{:S(2)}, u32[]{:S(2)}) %all-to-all-start.1) | async-done | bytes 655392 | tf_op jit(solution)/shard_map/all_to_all | solution.py:102
  82.7 0.4 abs_reduce_fusion
  83.2 0.1 reduce_max.36
  83.3 0.2 reduce_max.37
  83.5 0.7 fusion
  84.2 0.7 fusion.1
  84.9 0.2 div.37
  85.2 1.6 %div.38 = f32[80,4096]{1,0:T(8,128)} reshape(f32[80,8,4,128]{3,2,1,0:T(4,128)S(1)} %div.37) | data formatting | bytes 2621440 | tf_op jit(solution)/shard_map/div | solution.py:36
  86.8 0.2 copy.24
  87.0 1.1 %copy-done = f32[80,4096]{1,0:T(8,128)S(1)} copy-done((f32[80,4096]{1,0:T(8,128)S(1)}, f32[80,4096]{1,0:T(8,128)}, u32[]{:S(2)}) %copy-start) | copy-done | bytes 1310744
  88.1 0.3 convolution_convert_fusion.2
  88.4 0.0 copy-start.2
  88.5 0.0 copy-start.3
  88.5 0.2 copy.25
  88.7 0.8 copy-done.2
  89.5 0.2 copy-done.3
  89.7 1.3 %slice_select_fusion = (bf16[79,8,512]{2,1,0:T(8,128)(2,1)}, bf16[79,8,512]{2,1,0:T(8,128)(2,1)}) fusion(bf16[79,8,512]{2,1,0:T(8,128)(2,1)S(1)} %copy-done.2, bf16[80,8,512]{2,1,0:T(8,128)(2,1)S(1)} %bitcast.36, pred[79]{0:T(512)(128)(4,1)S(1)} %broadcast_compare_fusion.1, bf16[79,8,512]{2,1,0:T(8,128)(2,1)S(1)} %copy-done.3, ...), kind=kLoop, calls=%fused_computation.16 | loop fusion | flops 647168 | bytes 3883087 | tf_op jit(solution)/shard_map/jit(_where)/select_n | solution.py:129
  (23 shorter events, 0.1 us)
Async XLA Ops:
  7.2 23.9 %reduce-scatter.3.cloned.1.call-start = ((), (), s32[]{:S(2)}) async-start(), calls=%async_computation.4 | async-start | bytes 3145728 | tf_op jit(solution)/shard_map/reduce_scatter | solution.py:68
  17.7 27.0 %reduce-scatter.5.cloned.1.call-start = ((), (), s32[]{:S(2)}) async-start(), calls=%async_computation.5 | async-start | bytes 3145728 | tf_op jit(solution)/shard_map/reduce_scatter | solution.py:69
  28.2 0.7 copy-start.8
  28.2 0.9 copy-start.4
  28.2 1.7 %copy-start.11 = (s32[16]{0:T(128)S(1)}, s32[16]{0:T(128)}, u32[]{:S(2)}) copy-start(s32[16]{0:T(128)} %param.19) | copy-start | bytes 196
  28.2 2.8 %copy-start.6 = (f32[512]{0:T(512)S(1)}, f32[512]{0:T(512)}, u32[]{:S(2)}) copy-start(f32[512]{0:T(512)} %param.16) | copy-start | bytes 6148
  35.0 9.5 %copy-start.5 = (s32[1024]{0:T(1024)S(1)}, s32[1024]{0:T(1024)}, u32[]{:S(2)}) copy-start(s32[1024]{0:T(1024)} %param.21) | copy-start | bytes 12292
  35.0 9.6 %copy-start.7 = (f32[512]{0:T(512)S(1)}, f32[512]{0:T(512)}, u32[]{:S(2)}) copy-start(f32[512]{0:T(512)} %param.17) | copy-start | bytes 6148
  36.1 25.7 %all-to-all-start = ((bf16[16,5,8,512]{3,2,1,0:T(8,128)(2,1)}), bf16[16,5,8,512]{3,2,1,0:T(8,128)(2,1)S(1)}, u32[]{:S(2)}, u32[]{:S(2)}) async-start(bf16[16,5,8,512]{3,2,1,0:T(8,128)(2,1)} %bitcast.3), calls=%async_computation.1 | async-start | bytes 1310720 | tf_op jit(solution)/shard_map/all_to_all | solution.py:101
  61.8 20.9 %all-to-all-start.1 = ((bf16[16,5,8,512]{3,2,1,0:T(8,128)(2,1)}), bf16[16,5,8,512]{3,2,1,0:T(8,128)(2,1)S(1)}, u32[]{:S(2)}, u32[]{:S(2)}) async-start(bf16[16,5,8,512]{3,2,1,0:T(8,128)(2,1)} %bitcast.12), calls=%async_computation.3 | async-start | bytes 1310720 | tf_op jit(solution)/shard_map/all_to_all | solution.py:102
  69.2 1.3 %copy-start.1 = (f32[80,4096]{1,0:T(8,128)S(1)}, f32[80,4096]{1,0:T(8,128)}, u32[]{:S(2)}) copy-start(f32[80,4096]{1,0:T(8,128)} %div.35) | copy-start | bytes 3932164
  70.9 12.6 %copy-start.9 = (bf16[79,4]{0,1:T(4,128)(2,1)S(1)}, bf16[79,4]{0,1:T(4,128)(2,1)}, u32[]{:S(2)}) copy-start(bf16[79,4]{0,1:T(4,128)(2,1)} %param.24) | copy-start | bytes 1900
  70.9 13.3 %copy-start.10 = (bf16[79,4]{0,1:T(4,128)(2,1)S(1)}, bf16[79,4]{0,1:T(4,128)(2,1)}, u32[]{:S(2)}) copy-start(bf16[79,4]{0,1:T(4,128)(2,1)} %param.25) | copy-start | bytes 1900
  86.8 1.3 %copy-start = (f32[80,4096]{1,0:T(8,128)S(1)}, f32[80,4096]{1,0:T(8,128)}, u32[]{:S(2)}) copy-start(f32[80,4096]{1,0:T(8,128)} %div.38) | copy-start | bytes 3932164
  88.4 1.1 %copy-start.2 = (bf16[79,8,512]{2,1,0:T(8,128)(2,1)S(1)}, bf16[79,8,512]{2,1,0:T(8,128)(2,1)}, u32[]{:S(2)}) copy-start(bf16[79,8,512]{2,1,0:T(8,128)(2,1)} %param.23) | copy-start | bytes 1941508
  88.5 1.3 %copy-start.3 = (bf16[79,8,512]{2,1,0:T(8,128)(2,1)S(1)}, bf16[79,8,512]{2,1,0:T(8,128)(2,1)}, u32[]{:S(2)}) copy-start(bf16[79,8,512]{2,1,0:T(8,128)(2,1)} %param.22) | copy-start | bytes 1941508
Sparse Core Ops, SparseCore 0:
  17.8 12.3 reduce-scatter.2
  32.4 10.8 reduce-scatter.4
where the time goes:
time: 98.4 us; the launch traced here: 97.9 us
  waiting for transfers between devices  25.8 us (26%)
  matrix products  24.1 us (24%)
  between operations  14.4 us (15%)
  starting transfers between devices  12.9 us (13%)
  local copies, waits for them, and re-layouts  11.9 us (12%)
  other arithmetic  8.74 us (9%)
    all_to_all x1, waiting for transfers between devices, shards(): lax.all_to_all(raw[0], 'seq', split_axis=0, concat_axis=0, tiled=True)  14.1 us
    all_to_all x1, waiting for transfers between devices, shards(): lax.all_to_all(raw[1], 'seq', split_axis=0, concat_axis=0, tiled=True)  11.6 us
    dot_general x1, matrix products, shards(): jnp.dot(hidden, value_weight, preferred_element_type=jnp.float32)  10.5 us
    dot_general x1, matrix products, shards(): key_part = jnp.dot(hidden, key_weight, preferred_element_type=jnp.float32)  10.4 us
    all_to_all x1, starting transfers between devices, shards(): lax.all_to_all(raw[0], 'seq', split_axis=0, concat_axis=0, tiled=True)  8.35 us
    unnamed x30, local copies, waits for them, and re-layouts  6.9 us
    all_to_all x1, starting transfers between devices, shards(): lax.all_to_all(raw[1], 'seq', split_axis=0, concat_axis=0, tiled=True)  4.47 us
    div x4, local copies, waits for them, and re-layouts, normalize(): pages.astype(jnp.float32) / scale.astype(jnp.float32)[:, None, :, None]  3.66 us
  transfers between devices with their start and end apart: 4, of which 2 were waited for; matrix products, arithmetic and copies ran while one was open for 25% of the time, Pallas kernels for 0%

commit v1 on v0

v1 whole, which is shorter than its diff:
```python
import functools

import jax
import jax.numpy as jnp
from jax import lax
from jax.experimental import pallas as pl
from jax.experimental.pallas import tpu as pltpu
from jax.sharding import PartitionSpec as P

rope_base = 1000000.0
eps = 1e-06
KS = 4
MESH = pl.DeviceIdType.MESH


def body(
    n, cap, heads, hd, page,
    dk_ref, sr_ref, cos_ref, sin_ref, kb_ref, vb_ref, oks_ref, ovs_ref,
    h_hbm, kw_hbm, vw_hbm, kc_hbm, vc_hbm,
    kc_out, vc_out, ks_out, vs_out,
    h_v, w_v, p_v, u_v, part_s, part_r, own_v, bias_v, send_v, recv_v, cache_v, scale_v,
    h_sem, w_sem, c_sem, o_sem, ps_sem, pr_sem, s_sem, r_sem, l_sem,
):
    toks, kd = h_v.shape[1:]
    depth = KS * kd
    wide = 2 * hd
    half_cols = heads * hd
    per = half_cols // wide
    chunks = 2 * per

    me = lax.axis_index("seq")
    side = lax.axis_index("head")
    other = 1 - side
    slots = cache_v.shape[1]

    def w_copy(c, o, s):
        src = vw_hbm if c < per else kw_hbm
        col = (other if o == 0 else side) * half_cols + (c % per) * wide
        col = pl.multiple_of(col, wide)
        return pltpu.make_async_copy(
            src.at[pl.ds(s * kd, kd), pl.ds(col, wide)],
            w_v.at[c, o, pl.ds(s * kd, kd)],
            w_sem.at[c, o, s],
        )

    def h_copy(s):
        return pltpu.make_async_copy(
            h_hbm.at[:, pl.ds(s * kd, kd)], h_v.at[s], h_sem.at[s]
        )

    def cache_in(c):
        src = vc_hbm if c < per else kc_hbm
        return pltpu.make_async_copy(
            src.at[:, :, pl.ds((c % per) * wide, wide)], cache_v.at[c], c_sem.at[c]
        )

    def cache_out(c):
        dst = vc_out if c < per else kc_out
        return pltpu.make_async_copy(
            cache_v.at[c], dst.at[:, :, pl.ds((c % per) * wide, wide)], o_sem.at[c]
        )

    for s in range(KS):
        h_copy(s).start()
        w_copy(0, 0, s).start()
    for c in range(chunks):
        for o in range(2):
            if (c, o) != (0, 0):
                for s in range(KS):
                    w_copy(c, o, s).start()
    for c in range(chunks):
        cache_in(c).start()

    barrier = pltpu.get_barrier_semaphore()
    pl.semaphore_signal(barrier, inc=1, device_id={"head": other}, device_id_type=MESH)

    def greet(k, carry):
        pl.semaphore_signal(
            barrier, inc=1, device_id={"seq": lax.rem(me + k, n)}, device_id_type=MESH
        )
        return carry

    lax.fori_loop(1, n, greet, 0)

    for c in range(chunks):
        src = vb_ref if c < per else kb_ref
        bias_v[c] = src[:, pl.ds((c % per) * wide, wide)]
    rows = lax.broadcasted_iota(jnp.int32, p_v.shape, 0)
    p_v[...] = (rows == dk_ref[...]).astype(jnp.float32).astype(jnp.bfloat16)
    lanes = lax.broadcasted_iota(jnp.int32, u_v.shape, 1)
    u_v[...] = (lanes == sr_ref[...]).astype(jnp.float32).astype(jnp.bfloat16)
    scale_v[...] = jnp.zeros_like(scale_v)

    def partial(c, o, out, first):
        def step(s, carry):
            @pl.when(jnp.logical_and(c == 0, first))
            def _():
                pltpu.make_async_copy(h_v.at[s], h_v.at[s], h_sem.at[s]).wait()

            w_slice = w_v.at[c, o, pl.ds(pl.multiple_of(s * kd, kd), kd)]
            pltpu.make_async_copy(w_slice, w_slice, w_sem.at[c, o, s]).wait()
            got = jnp.dot(h_v[s], w_slice[...], preferred_element_type=jnp.float32)

            @pl.when(s == 0)
            def _():
                out[...] = got

            @pl.when(s > 0)
            def _():
                out[...] = out[...] + got

            return carry

        lax.fori_loop(0, KS, step, 0)

    def produce(c, carry):
        partial(c, 0, part_s.at[c], True)

        @pl.when(c == 0)
        def _():
            pl.semaphore_wait(barrier, n)

        swap = pltpu.make_async_remote_copy(
            src_ref=part_s.at[c],
            dst_ref=part_r.at[c],
            send_sem=ps_sem.at[c],
            recv_sem=pr_sem.at[c],
            device_id={"head": other},
            device_id_type=MESH,
        )
        swap.start()
        partial(c, 1, own_v, False)
        swap.wait()
        total = own_v[...] + part_r[c] + bias_v[c]
        is_key = c >= per
        cosine = jnp.where(is_key, cos_ref[...], 1.0)
        sine = jnp.where(is_key, sin_ref[...], 0.0)
        pieces = []
        for j in range(2):
            x = total[:, j * hd:(j + 1) * hd]
            pieces.append(x * cosine + pltpu.roll(x, hd // 2, 1) * sine)
        rounded = jnp.concatenate(pieces, axis=1).astype(jnp.bfloat16)
        placed = jnp.dot(p_v[...], rounded, preferred_element_type=jnp.float32)
        left = placed[:, :hd].reshape(n * cap, page, hd)
        right = placed[:, hd:].reshape(n * cap, page, hd)
        send_v[c] = jnp.concatenate([left, right], axis=1).astype(jnp.bfloat16)
        pltpu.make_async_copy(
            send_v.at[c, pl.ds(0, cap)], recv_v.at[c, pl.ds(0, cap)], l_sem.at[c]
        ).start()

        def send(j, carry2):
            k = n // 2 + (1 - 2 * (j % 2)) * ((j + 1) // 2)
            pltpu.make_async_remote_copy(
                src_ref=send_v.at[c, pl.ds(k * cap, cap)],
                dst_ref=recv_v.at[c, pl.ds(k * cap, cap)],
                send_sem=s_sem.at[c],
                recv_sem=r_sem.at[c],
                device_id={"seq": lax.rem(me + k, n)},
                device_id_type=MESH,
            ).start()
            return carry2

        lax.fori_loop(0, n - 1, send, 0)
        return carry

    lax.fori_loop(0, chunks, produce, 0)

    head_lane = lax.broadcasted_iota(jnp.int32, (1, 1, hd), 2)
    sr = sr_ref[...]
    written = (sr >= 0)[: slots * page]

    def consume(c, carry):
        pltpu.make_async_copy(
            recv_v.at[c, pl.ds(0, cap)], recv_v.at[c, pl.ds(0, cap)], l_sem.at[c]
        ).wait()
        rest = recv_v.at[c, pl.ds(cap, (n - 1) * cap)]
        pltpu.make_async_copy(rest, rest, r_sem.at[c]).wait()
        pltpu.make_async_copy(cache_v.at[c], cache_v.at[c], c_sem.at[c]).wait()
        got = recv_v[c].astype(jnp.float32)
        coded = []
        for j in range(2):
            x = got[:, j * page:(j + 1) * page, :]
            largest = jnp.max(jnp.max(jnp.abs(x), axis=1, keepdims=True), axis=2, keepdims=True)
            scale = (largest + eps).astype(jnp.bfloat16).astype(jnp.float32)
            scale_v[...] += jnp.where(head_lane == 2 * c + j, scale, 0.0)
            coded.append((x / scale).reshape(n * cap * page, hd))
        codes = jnp.concatenate(coded, axis=1).astype(jnp.bfloat16)
        placed = jnp.dot(u_v[...], codes, preferred_element_type=jnp.float32)
        placed = placed[: slots * page]
        old = cache_v[c].astype(jnp.float32).reshape(slots * page, wide)
        cache_v[c] = (
            jnp.where(written, placed, old).reshape(slots, page, wide).astype(jnp.bfloat16)
        )
        for i in range(chunks):
            @pl.when(c == i)
            def _():
                cache_out(i).start()
        return carry

    lax.fori_loop(0, chunks, consume, 0)

    flat = jnp.broadcast_to(scale_v[...], (n * cap, page, hd)).reshape(n * cap * page, hd)
    spread = jnp.dot(u_v[...], flat.astype(jnp.bfloat16), preferred_element_type=jnp.float32)
    spread = spread[: slots * page].reshape(slots, page, hd)[:, 0, :]
    hit = jnp.max(
        jnp.where(written, 1.0, 0.0).reshape(slots, page, 1), axis=1
    ) > 0.5
    vs_out[...] = jnp.where(
        hit, spread[:, :heads], ovs_ref[...].astype(jnp.float32)
    ).astype(jnp.bfloat16)
    ks_out[...] = jnp.where(
        hit, spread[:, heads:2 * heads], oks_ref[...].astype(jnp.float32)
    ).astype(jnp.bfloat16)

    for c in range(chunks):
        cache_out(c).wait()
        out = send_v.at[c, pl.ds(cap, (n - 1) * cap)]
        pltpu.make_async_copy(out, out, s_sem.at[c]).wait()


def shards(
    hidden,
    key_weight,
    value_weight,
    key_bias,
    value_bias,
    request_tokens,
    request_context,
    page_owner,
    page_slot,
    key_cache,
    value_cache,
    stored_key_scales,
    value_scales,
):
    toks, depth = hidden.shape
    slots, page, cols = key_cache.shape
    heads = stored_key_scales.shape[1]
    hd = cols // heads
    pages_here = toks // page
    n = lax.axis_size("seq")
    me = lax.axis_index("seq")
    cap = (pages_here + n - 1) // n + 1
    half = hd // 2
    rows = n * cap * page
    srows = (slots * page + 15) // 16 * 16

    ends = jnp.cumsum(request_tokens)
    starts = ends - request_tokens
    token_ids = me * toks + jnp.arange(toks)
    inside = (token_ids[:, None] >= starts[None, :]) & (token_ids[:, None] < ends[None, :])
    offset = jnp.sum(jnp.where(inside, (request_context - starts)[None, :], 0), axis=1)
    positions = (offset + token_ids).astype(jnp.float32)
    freqs = jnp.exp(
        -jnp.log(jnp.float32(rope_base)) * (2.0 * jnp.arange(half).astype(jnp.float32) / hd)
    )
    angle = positions[:, None] * freqs[None, :]
    cosine, sine = jnp.cos(angle), jnp.sin(angle)
    cos_t = jnp.concatenate([cosine, cosine], axis=1)
    sin_t = jnp.concatenate([-sine, sine], axis=1)

    owners = page_owner.reshape(n, pages_here)
    within = jnp.arange(pages_here)
    before = (owners[:, :, None] == owners[:, None, :]) & (
        within[None, None, :] < within[None, :, None]
    )
    rank = jnp.sum(before.astype(jnp.int32), axis=2)
    own_owner = lax.dynamic_index_in_dim(owners, me, 0, keepdims=False)
    own_rank = lax.dynamic_index_in_dim(rank, me, 0, keepdims=False)
    place = lax.rem(own_owner - me + n, n) * cap + own_rank
    dk = (place[:, None] * page + jnp.arange(page)[None, :]).reshape(1, toks)
    senders = jnp.arange(n)
    lane = lax.rem(me - senders + n, n)[:, None] * cap + rank
    mine = owners == me
    hit = (page_slot.reshape(1, -1) == jnp.arange(srows // page)[:, None]) & mine.reshape(1, -1)
    src = jnp.sum(jnp.where(hit, lane.reshape(1, -1) + 1, 0), axis=1) - 1
    sr = jnp.where(
        src[:, None] >= 0, src[:, None] * page + jnp.arange(page)[None, :], -1
    ).reshape(srows, 1)

    wide = 2 * hd
    chunks = 2 * (cols // wide)
    vm = pl.BlockSpec(memory_space=pltpu.VMEM)
    hbm = pl.BlockSpec(memory_space=pl.ANY)
    f32, b16 = jnp.float32, jnp.bfloat16
    return pl.pallas_call(
        functools.partial(body, n, cap, heads, hd, page),
        out_shape=(
            jax.ShapeDtypeStruct(key_cache.shape, b16),
            jax.ShapeDtypeStruct(value_cache.shape, b16),
            jax.ShapeDtypeStruct(stored_key_scales.shape, b16),
            jax.ShapeDtypeStruct(value_scales.shape, b16),
        ),
        in_specs=[vm] * 8 + [hbm] * 5,
        out_specs=(hbm, hbm, vm, vm),
        scratch_shapes=[
            pltpu.VMEM((KS, toks, depth // KS), b16),
            pltpu.VMEM((chunks, 2, depth, wide), b16),
            pltpu.VMEM((rows, toks), b16),
            pltpu.VMEM((srows, rows), b16),
            pltpu.VMEM((chunks, toks, wide), f32),
            pltpu.VMEM((chunks, toks, wide), f32),
            pltpu.VMEM((toks, wide), f32),
            pltpu.VMEM((chunks, 1, wide), f32),
            pltpu.VMEM((chunks, n * cap, 2 * page, hd), b16),
            pltpu.VMEM((chunks, n * cap, 2 * page, hd), b16),
            pltpu.VMEM((chunks, slots, page, wide), b16),
            pltpu.VMEM((n * cap, 1, hd), f32),
            pltpu.SemaphoreType.DMA((KS,)),
            pltpu.SemaphoreType.DMA((chunks, 2, KS)),
            pltpu.SemaphoreType.DMA((chunks,)),
            pltpu.SemaphoreType.DMA((chunks,)),
            pltpu.SemaphoreType.DMA((chunks,)),
            pltpu.SemaphoreType.DMA((chunks,)),
            pltpu.SemaphoreType.DMA((chunks,)),
            pltpu.SemaphoreType.DMA((chunks,)),
            pltpu.SemaphoreType.DMA((chunks,)),
        ],
        compiler_params=pltpu.CompilerParams(
            collective_id=0, has_side_effects=True, vmem_limit_bytes=60 * 1024 * 1024
        ),
    )(
        dk, sr, cos_t, sin_t, key_bias.reshape(1, -1), value_bias.reshape(1, -1),
        stored_key_scales, value_scales, hidden, key_weight, value_weight,
        key_cache, value_cache,
    )


def solution(mesh):
    placed = (
        P("seq", "head"),
        P("head", None),
        P("head", None),
        P("head"),
        P("head"),
        P(),
        P(),
        P(),
        P(),
        P("seq", None, "head"),
        P("seq", None, "head"),
        P("seq", "head"),
        P("seq", "head"),
    )
    return jax.shard_map(
        shards,
        mesh=mesh,
        in_specs=placed,
        out_specs=(
            P("seq", None, "head"),
            P("seq", None, "head"),
            P("seq", "head"),
            P("seq", "head"),
        ),
        check_vma=False,
    )
```

time: 98.4 us -> 67.7 us (0.69)
  Pallas kernels: 0 us -> 48.6 us
  waiting for transfers between devices: 25.8 us -> 0 us
  matrix products: 24.1 us -> 0 us
  between operations: 14.4 us -> 0.71 us
  starting transfers between devices: 12.9 us -> 0 us
  other arithmetic: 8.74 us -> 5.29 us
    pallas_call x0 -> x1, Pallas kernels: none -> 48.6 us  [shards(): pl.pallas_call(functools.partial(body, n, cap, heads, hd, page), out_shap...]
    all_to_all x2 -> x0, waiting for transfers between devices: 25.8 us -> none  [the longest x1 14.1 us: shards(): lax.all_to_all(raw[0], 'seq', split_axis=0, concat_axis=0, tiled=True)]
    dot_general x9 -> x0, matrix products: 24.1 us -> none  [the longest x1 10.5 us: shards(): jnp.dot(hidden, value_weight, preferred_element_type=jnp.float32)]
    all_to_all x2 -> x0, starting transfers between devices: 12.8 us -> none  [the longest x1 8.35 us: shards(): lax.all_to_all(raw[0], 'seq', split_axis=0, concat_axis=0, tiled=True)]
    div x4 -> x0, local copies, waits for them, and re-layouts: 3.66 us -> none  [normalize(): pages.astype(jnp.float32) / scale.astype(jnp.float32)[:, None, :, None]]
    pallas_call x0 -> x2, local copies, waits for them, and re-layouts: none -> 2.75 us  [shards(): pl.pallas_call(functools.partial(body, n, cap, heads, hd, page), out_shap...]
    convert_element_type x4 -> x1, other arithmetic: 1.37 us -> 0.01 us  [shards(): positions = (offset + token_ids).astype(jnp.float32)]
    add x4 -> x3, other arithmetic: 1.44 us -> 0.15 us  [the longest x1 0.07 us: shards(): src = jnp.sum(jnp.where(hit, lane.reshape(1, -1) + 1, 0), axis=1) - 1]
  transfers between devices with their start and end apart: 4 -> 0, of which waited for: 2 -> 0; matrix products, arithmetic and copies ran while one was open for 25% -> 0% of each run, Pallas kernels for 0% -> 0%
where the time goes in v1:
time: 67.7 us; the launch traced here: 67.2 us
  Pallas kernels  48.6 us (72%)
  local copies, waits for them, and re-layouts  12.5 us (18%)
  other arithmetic  5.29 us (8%)
  between operations  0.71 us (1%)
    pallas_call x1, Pallas kernels, shards(): pl.pallas_call(functools.partial(body, n, cap, heads, hd, page), out_shap...  48.6 us
    unnamed x4, local copies, waits for them, and re-layouts  6.69 us
    pallas_call x2, local copies, waits for them, and re-layouts, shards(): pl.pallas_call(functools.partial(body, n, cap, heads, hd, page), out_shap...  2.75 us

profile of v1, /device:TPU:0, one launch (start us, length us, event | category | flops | bytes accessed | tf_op | source)
XLA Modules:
  0.0 67.2 jit_solution(4647307391385403480)
XLA Ops:
  0.7 0.7 %broadcast_compare_fusion = pred[1024]{0:T(1024)(128)(4,1)S(1)} fusion(s32[1024]{0:T(1024)} %param.20, s32[]{:T(128)S(6)} %axis_index.15), kind=kLoop, calls=%fused_computation.20 | loop fusion | flops 1024 | bytes 5124 | tf_op jit(solution)/shard_map/eq | solution.py:274
  1.4 0.8 %reshape.205 = s32[16,64]{1,0:T(8,128)S(1)} reshape(s32[1024]{0:T(1024)} %param.20) | data formatting | bytes 8192 | tf_op jit(solution)/shard_map/reshape | solution.py:262
  2.1 0.7 %copy.28 = s32[16,1]{1,0:T(8,128)S(1)} copy(s32[16,1]{0,1:T(1,128)} %bitcast.11) | data formatting | bytes 128 | tf_op jit(solution)/shard_map/reshape.176
  2.9 0.1 reduce
  3.0 0.7 %fusion.8 = (s32[16]{0:T(128)S(1)}, s32[16]{0:T(128)S(1)}) fusion(s32[16]{0:T(128)} %param.19, s32[16]{0:T(128)S(1)} %reduce, s32[16]{0:T(128)} %param.18), kind=kLoop, calls=%fused_computation.30 | loop fusion | flops 32 | bytes 320 | tf_op jit(solution)/shard_map/sub | solution.py:252
  3.7 0.1 select_reduce_fusion.1
  3.8 0.5 convert_reduce_fusion
  4.3 0.1 add_add_fusion
  4.4 0.1 add.142
  4.5 0.9 %select_reduce_fusion = s32[80]{0:T(128)S(1)} fusion(s32[1024]{0:T(1024)S(1)} %add.142, s32[1024]{0:T(1024)} %param.21, pred[1024]{0:T(1024)(128)(4,1)S(1)} %broadcast_compare_fusion), kind=kLoop, calls=%fused_computation.3 | loop fusion | flops 327600 | bytes 9536 | tf_op jit(solution)/shard_map/reduce_sum | solution.py:276
  5.4 1.4 %copy.30.oks_ref = bf16[79,4]{1,0:T(8,128)(2,1)} copy(bf16[79,4]{0,1:T(4,128)(2,1)} %param.24) | data formatting | bytes 1264 | tf_op args[11]
  6.8 1.4 %copy.31.ovs_ref = bf16[79,4]{1,0:T(8,128)(2,1)} copy(bf16[79,4]{0,1:T(4,128)(2,1)} %param.25) | data formatting | bytes 1264 | tf_op args[12]
  8.2 0.1 iota_add_fusion
  8.2 0.7 %add.136.dk_ref = s32[1,512]{1,0:T(1,128)} reshape(s32[64,8]{1,0:T(8,128)S(1)} %iota_add_fusion) | data formatting | bytes 4096 | tf_op jit(solution)/shard_map/add | solution.py:271
  8.9 0.1 add_select_fusion
  9.0 0.9 %select_n.32.sr_ref = s32[640,1]{1,0:T(8,128)} reshape(s32[80,8]{1,0:T(8,128)S(1)} %add_select_fusion) | data formatting | bytes 5120 | tf_op jit(solution)/shard_map/jit(_where)/select_n | solution.py:277
  9.9 1.0 %fusion.1 = (f32[512,64]{1,0:T(8,128)S(1)}, f32[512,64]{1,0:T(8,128)S(1)}, f32[512,64]{1,0:T(8,128)S(1)}) fusion(f32[64]{0:T(128)S(1)} %multiply_exponential_fusion, f32[512]{0:T(512)S(1)} %add_convert_fusion), kind=kLoop, calls=%fused_computation.8 | loop fusion | flops 65536 | bytes 395520 | tf_op jit(solution)/shard_map/neg | solution.py:260
  10.9 1.0 %pad_maximum_fusion = (f32[512,128]{1,0:T(8,128)}, f32[512,128]{1,0:T(8,128)}) fusion(f32[512,64]{1,0:T(8,128)S(1)} %get-tuple-element.20, f32[512,64]{1,0:T(8,128)S(1)} %get-tuple-element.19, f32[512,64]{1,0:T(8,128)S(1)} %get-tuple-element.18), kind=kLoop, calls=%fused_computation.6 | loop fusion | flops 131072 | bytes 917504 | tf_op jit(solution)/shard_map/concatenate | solution.py:259
  11.9 48.6 %shard_map.156 = (bf16[79,8,512]{2,1,0:T(8,128)(2,1)}, bf16[79,8,512]{2,1,0:T(8,128)(2,1)}, bf16[79,4]{1,0:T(8,128)(2,1)}, bf16[79,4]{1,0:T(8,128)(2,1)}) custom-call(s32[1,512]{1,0:T(1,128)} %add.136.dk_ref, s32[640,1]{1,0:T(8,128)} %select_n.32.sr_ref, f32[512,128]{1,0:T(8,128)} %get-tuple-element.21.cos_ref, f32[512,128]{1,0:T(8,128)} %get-tuple-element.22.sin_ref, ...), custom_call_target="tpu_custom_call" | custom-call | tf_op jit(solution)/shard_map/pallas_call | solution.py:286
  60.5 1.4 %copy.32 = bf16[79,4]{0,1:T(4,128)(2,1)} copy(bf16[79,4]{1,0:T(8,128)(2,1)} %get-tuple-element.14) | data formatting | bytes 1264 | tf_op jit(solution)/shard_map/pallas_call | solution.py:286
  61.9 1.4 %copy.33 = bf16[79,4]{0,1:T(4,128)(2,1)} copy(bf16[79,4]{1,0:T(8,128)(2,1)} %get-tuple-element.15) | data formatting | bytes 1264 | tf_op jit(solution)/shard_map/pallas_call | solution.py:286
  63.3 2.0 %copy.36 = bf16[79,8,512]{2,1,0:T(8,128)(2,1)} copy(bf16[79,8,512]{2,1,0:T(8,128)(2,1)} %get-tuple-element.27) | data formatting | bytes 1294336
  65.2 2.0 %copy.37 = bf16[79,8,512]{2,1,0:T(8,128)(2,1)} copy(bf16[79,8,512]{2,1,0:T(8,128)(2,1)} %get-tuple-element.28) | data formatting | bytes 1294336
  (9 shorter events, 0.1 us)

commit v2 on v1

--- a/solution.py
+++ b/solution.py
@@ -15,11 +15,13 @@
 
 def body(
     n, cap, heads, hd, page,
-    dk_ref, sr_ref, cos_ref, sin_ref, kb_ref, vb_ref, oks_ref, ovs_ref,
+    own_in, slot_in, freq_in, kb_in, vb_in, oks_in, ovs_in, rt_in, rc_in,
     h_hbm, kw_hbm, vw_hbm, kc_hbm, vc_hbm,
     kc_out, vc_out, ks_out, vs_out,
     h_v, w_v, p_v, u_v, part_s, part_r, own_v, bias_v, send_v, recv_v, cache_v, scale_v,
-    h_sem, w_sem, c_sem, o_sem, ps_sem, pr_sem, s_sem, r_sem, l_sem,
+    cos_v, sin_v, sr_v,
+    own_ref, slot_ref, freq_ref, kb_ref, vb_ref, oks_ref, ovs_ref, rt_ref, rc_ref,
+    h_sem, w_sem, c_sem, o_sem, ps_sem, pr_sem, s_sem, r_sem, l_sem, i_sem,
 ):
     toks, kd = h_v.shape[1:]
     depth = KS * kd
@@ -60,16 +62,20 @@
             cache_v.at[c], dst.at[:, :, pl.ds((c % per) * wide, wide)], o_sem.at[c]
         )
 
+    pairs = (
+        (own_in, own_ref), (slot_in, slot_ref), (freq_in, freq_ref), (kb_in, kb_ref),
+        (vb_in, vb_ref), (oks_in, oks_ref), (ovs_in, ovs_ref), (rt_in, rt_ref), (rc_in, rc_ref),
+    )
+    small = [
+        pltpu.make_async_copy(src, dst, i_sem.at[i]) for i, (src, dst) in enumerate(pairs)
+    ]
+    for copy in small:
+        copy.start()
     for s in range(KS):
         h_copy(s).start()
         w_copy(0, 0, s).start()
-    for c in range(chunks):
-        for o in range(2):
-            if (c, o) != (0, 0):
-                for s in range(KS):
-                    w_copy(c, o, s).start()
-    for c in range(chunks):
-        cache_in(c).start()
+    for s in range(KS):
+        w_copy(0, 1, s).start()
 
     barrier = pltpu.get_barrier_semaphore()
     pl.semaphore_signal(barrier, inc=1, device_id={"head": other}, device_id_type=MESH)
@@ -81,14 +87,67 @@
         return carry
 
     lax.fori_loop(1, n, greet, 0)
+    for copy in small:
+        copy.wait()
 
     for c in range(chunks):
         src = vb_ref if c < per else kb_ref
         bias_v[c] = src[:, pl.ds((c % per) * wide, wide)]
-    rows = lax.broadcasted_iota(jnp.int32, p_v.shape, 0)
-    p_v[...] = (rows == dk_ref[...]).astype(jnp.float32).astype(jnp.bfloat16)
-    lanes = lax.broadcasted_iota(jnp.int32, u_v.shape, 1)
-    u_v[...] = (lanes == sr_ref[...]).astype(jnp.float32).astype(jnp.bfloat16)
+    total_pages = own_ref.shape[1]
+    here = total_pages // n
+    f32 = jnp.float32
+    owner = own_ref[...]
+    gid = lax.broadcasted_iota(jnp.int32, (1, total_pages), 1)
+    within = gid % here
+    match = lax.broadcasted_iota(jnp.int32, (n, total_pages), 0) == owner
+    count = jnp.where(match, 1.0, 0.0)
+    shift = 1
+    while shift < here:
+        count = count + jnp.where(within >= shift, pltpu.roll(count, shift, 1), 0.0)
+        shift *= 2
+    rank = jnp.sum(jnp.where(match, count, 0.0), axis=0, keepdims=True) - 1.0
+    place = ((owner - me + n) % n * cap).astype(f32) + rank
+    place = pltpu.roll(
+        jnp.broadcast_to(place, (8, total_pages)), (total_pages - me * here) % total_pages, 1
+    )[:, :here]
+    expand = (
+        lax.broadcasted_iota(jnp.int32, (here, toks), 0)
+        == lax.broadcasted_iota(jnp.int32, (here, toks), 1) // page
+    )
+    place = jnp.dot(
+        place.astype(jnp.bfloat16),
+        jnp.where(expand, 1.0, 0.0).astype(jnp.bfloat16),
+        preferred_element_type=f32,
+    )[:1]
+    token = lax.broadcasted_iota(jnp.int32, (1, toks), 1)
+    dk = place * page + (token % page).astype(f32)
+    rows = lax.broadcasted_iota(jnp.int32, p_v.shape, 0).astype(f32)
+    p_v[...] = jnp.where(rows == dk, 1.0, 0.0).astype(jnp.bfloat16)
+
+    def unpack_table():
+        slot = jnp.where(owner == me, slot_ref[...], -1)
+        lane = (((me - gid // here + n) % n) * cap).astype(f32) + rank + 1.0
+        want = lax.broadcasted_iota(jnp.int32, (u_v.shape[0], 1), 0)
+        src = jnp.sum(jnp.where(want // page == slot, lane, 0.0), axis=1, keepdims=True) - 1.0
+        sr_v[...] = jnp.where(src >= 0.0, src * page + (want % page).astype(f32), -1.0)
+        lanes = lax.broadcasted_iota(jnp.int32, u_v.shape, 1).astype(f32)
+        u_v[...] = jnp.where(lanes == sr_v[...], 1.0, 0.0).astype(jnp.bfloat16)
+
+    def rope_table():
+        token_ids = me * toks + lax.broadcasted_iota(jnp.int32, cos_v.shape, 0)
+        offset = jnp.zeros_like(token_ids)
+        start = jnp.int32(0)
+        for r in range(rt_ref.shape[0]):
+            offset = jnp.where(token_ids >= start, rc_ref[r] - start, offset)
+            start = start + rt_ref[r]
+        angle = (offset + token_ids).astype(f32) * freq_ref[...]
+        cos_v[...] = jnp.cos(angle)
+        sine = jnp.sin(angle)
+        front = lax.broadcasted_iota(jnp.int32, cos_v.shape, 1) < hd // 2
+        sin_v[...] = jnp.where(front, -sine, sine)
+
+    cos_v[...] = jnp.ones_like(cos_v)
+    sin_v[...] = jnp.zeros_like(sin_v)
     scale_v[...] = jnp.zeros_like(scale_v)
 
     def partial(c, o, out, first):
@@ -114,6 +173,18 @@
         lax.fori_loop(0, KS, step, 0)
 
     def produce(c, carry):
+        for i in range(1, chunks):
+            @pl.when(c == i - 1)
+            def _():
+                for o in range(2):
+                    for s in range(KS):
+                        w_copy(i, o, s).start()
+
+        @pl.when(c == chunks - 2)
+        def _():
+            for i in range(chunks):
+                cache_in(i).start()
+
         partial(c, 0, part_s.at[c], True)
 
         @pl.when(c == 0)
@@ -132,9 +203,8 @@
         partial(c, 1, own_v, False)
         swap.wait()
         total = own_v[...] + part_r[c] + bias_v[c]
-        is_key = c >= per
-        cosine = jnp.where(is_key, cos_ref[...], 1.0)
-        sine = jnp.where(is_key, sin_ref[...], 0.0)
+        cosine = cos_v[...]
+        sine = sin_v[...]
         pieces = []
         for j in range(2):
             x = total[:, j * hd:(j + 1) * hd]
@@ -161,13 +231,18 @@
             return carry2
 
         lax.fori_loop(0, n - 1, send, 0)
+
+        @pl.when(c == per - 1)
+        def _():
+            rope_table()
+
         return carry
 
     lax.fori_loop(0, chunks, produce, 0)
 
+    unpack_table()
     head_lane = lax.broadcasted_iota(jnp.int32, (1, 1, hd), 2)
-    sr = sr_ref[...]
-    written = (sr >= 0)[: slots * page]
+    written = (sr_v[...] >= 0.0)[: slots * page]
 
     def consume(c, carry):
         pltpu.make_async_copy(
@@ -202,20 +277,43 @@
     flat = jnp.broadcast_to(scale_v[...], (n * cap, page, hd)).reshape(n * cap * page, hd)
     spread = jnp.dot(u_v[...], flat.astype(jnp.bfloat16), preferred_element_type=jnp.float32)
     spread = spread[: slots * page].reshape(slots, page, hd)[:, 0, :]
-    hit = jnp.max(
-        jnp.where(written, 1.0, 0.0).reshape(slots, page, 1), axis=1
-    ) > 0.5
+    spread = jnp.concatenate([spread, jnp.zeros((128 - slots % 128, hd), f32)], axis=0)
+    spread = jnp.transpose(spread)[:, :slots]
     vs_out[...] = jnp.where(
-        hit, spread[:, :heads], ovs_ref[...].astype(jnp.float32)
+        spread[:heads] > 0.0, spread[:heads], ovs_ref[...].astype(f32)
     ).astype(jnp.bfloat16)
     ks_out[...] = jnp.where(
-        hit, spread[:, heads:2 * heads], oks_ref[...].astype(jnp.float32)
+        spread[heads:2 * heads] > 0.0, spread[heads:2 * heads], oks_ref[...].astype(f32)
     ).astype(jnp.bfloat16)
 
     for c in range(chunks):
         cache_out(c).wait()
         out = send_v.at[c, pl.ds(cap, (n - 1) * cap)]
         pltpu.make_async_copy(out, out, s_sem.at[c]).wait()
+
+
+def hand_on(pieces, *refs):
+    srcs, dsts, held = refs[:4], refs[4:8], refs[8:12]
+    in_sem, out_sem = refs[12:]
+    views = []
+    for src, dst, here in zip(srcs, dsts, held):
+        if src.shape[0] >= 8:
+            size = src.shape[0]
+            cuts = [size * i // pieces for i in range(pieces + 1)]
+            for low, high in zip(cuts, cuts[1:]):
+                part = pl.ds(low, high - low)
+                views.append((src.at[part], dst.at[part], here.at[part]))
+        else:
+            views.append((src, dst, here))
+    ins = [pltpu.make_async_copy(v[0], v[2], in_sem.at[i]) for i, v in enumerate(views)]
+    outs = [pltpu.make_async_copy(v[2], v[1], out_sem.at[i]) for i, v in enumerate(views)]
+    for copy in ins:
+        copy.start()
+    for copy_in, copy_out in zip(ins, outs):
+        copy_in.wait()
+        copy_out.start()
+    for copy in outs:
+        copy.wait()
 
 
 def shards(
@@ -239,59 +337,30 @@
     hd = cols // heads
     pages_here = toks // page
     n = lax.axis_size("seq")
-    me = lax.axis_index("seq")
     cap = (pages_here + n - 1) // n + 1
     half = hd // 2
     rows = n * cap * page
     srows = (slots * page + 15) // 16 * 16
 
-    ends = jnp.cumsum(request_tokens)
-    starts = ends - request_tokens
-    token_ids = me * toks + jnp.arange(toks)
-    inside = (token_ids[:, None] >= starts[None, :]) & (token_ids[:, None] < ends[None, :])
-    offset = jnp.sum(jnp.where(inside, (request_context - starts)[None, :], 0), axis=1)
-    positions = (offset + token_ids).astype(jnp.float32)
     freqs = jnp.exp(
         -jnp.log(jnp.float32(rope_base)) * (2.0 * jnp.arange(half).astype(jnp.float32) / hd)
     )
-    angle = positions[:, None] * freqs[None, :]
-    cosine, sine = jnp.cos(angle), jnp.sin(angle)
-    cos_t = jnp.concatenate([cosine, cosine], axis=1)
-    sin_t = jnp.concatenate([-sine, sine], axis=1)
-
-    owners = page_owner.reshape(n, pages_here)
-    within = jnp.arange(pages_here)
-    before = (owners[:, :, None] == owners[:, None, :]) & (
-        within[None, None, :] < within[None, :, None]
-    )
-    rank = jnp.sum(before.astype(jnp.int32), axis=2)
-    own_owner = lax.dynamic_index_in_dim(owners, me, 0, keepdims=False)
-    own_rank = lax.dynamic_index_in_dim(rank, me, 0, keepdims=False)
-    place = lax.rem(own_owner - me + n, n) * cap + own_rank
-    dk = (place[:, None] * page + jnp.arange(page)[None, :]).reshape(1, toks)
-    senders = jnp.arange(n)
-    lane = lax.rem(me - senders + n, n)[:, None] * cap + rank
-    mine = owners == me
-    hit = (page_slot.reshape(1, -1) == jnp.arange(srows // page)[:, None]) & mine.reshape(1, -1)
-    src = jnp.sum(jnp.where(hit, lane.reshape(1, -1) + 1, 0), axis=1) - 1
-    sr = jnp.where(
-        src[:, None] >= 0, src[:, None] * page + jnp.arange(page)[None, :], -1
-    ).reshape(srows, 1)
-
+    freqs = jnp.concatenate([freqs, freqs]).reshape(1, hd)
     wide = 2 * hd
     chunks = 2 * (cols // wide)
     vm = pl.BlockSpec(memory_space=pltpu.VMEM)
     hbm = pl.BlockSpec(memory_space=pl.ANY)
     f32, b16 = jnp.float32, jnp.bfloat16
-    return pl.pallas_call(
+    old_value_scales = value_scales
+    done = pl.pallas_call(
         functools.partial(body, n, cap, heads, hd, page),
         out_shape=(
             jax.ShapeDtypeStruct(key_cache.shape, b16),
             jax.ShapeDtypeStruct(value_cache.shape, b16),
-            jax.ShapeDtypeStruct(stored_key_scales.shape, b16),
-            jax.ShapeDtypeStruct(value_scales.shape, b16),
+            jax.ShapeDtypeStruct((heads, slots), b16),
+            jax.ShapeDtypeStruct((heads, slots), b16),
         ),
-        in_specs=[vm] * 8 + [hbm] * 5,
+        in_specs=[hbm] * 14,
         out_specs=(hbm, hbm, vm, vm),
         scratch_shapes=[
             pltpu.VMEM((KS, toks, depth // KS), b16),
@@ -306,6 +375,18 @@
             pltpu.VMEM((chunks, n * cap, 2 * page, hd), b16),
             pltpu.VMEM((chunks, slots, page, wide), b16),
             pltpu.VMEM((n * cap, 1, hd), f32),
+            pltpu.VMEM((toks, hd), f32),
+            pltpu.VMEM((toks, hd), f32),
+            pltpu.VMEM((srows, 1), f32),
+            pltpu.VMEM((1, page_owner.shape[0]), jnp.int32),
+            pltpu.VMEM((1, page_owner.shape[0]), jnp.int32),
+            pltpu.VMEM((1, hd), f32),
+            pltpu.VMEM((1, cols), f32),
+            pltpu.VMEM((1, cols), f32),
+            pltpu.VMEM((heads, slots), b16),
+            pltpu.VMEM((heads, slots), b16),
+            pltpu.SMEM(request_tokens.shape, jnp.int32),
+            pltpu.SMEM(request_tokens.shape, jnp.int32),
             pltpu.SemaphoreType.DMA((KS,)),
             pltpu.SemaphoreType.DMA((chunks, 2, KS)),
             pltpu.SemaphoreType.DMA((chunks,)),
@@ -315,15 +396,29 @@
             pltpu.SemaphoreType.DMA((chunks,)),
             pltpu.SemaphoreType.DMA((chunks,)),
             pltpu.SemaphoreType.DMA((chunks,)),
+            pltpu.SemaphoreType.DMA((9,)),
         ],
         compiler_params=pltpu.CompilerParams(
             collective_id=0, has_side_effects=True, vmem_limit_bytes=60 * 1024 * 1024
         ),
     )(
-        dk, sr, cos_t, sin_t, key_bias.reshape(1, -1), value_bias.reshape(1, -1),
-        stored_key_scales, value_scales, hidden, key_weight, value_weight,
-        key_cache, value_cache,
-    )
+        page_owner.reshape(1, -1), page_slot.reshape(1, -1), freqs,
+        key_bias.reshape(1, -1), value_bias.reshape(1, -1),
+        stored_key_scales.T, old_value_scales.T, request_tokens, request_context,
+        hidden, key_weight, value_weight, key_cache, value_cache,
+    )
+    pieces = 2
+    moves = 2 * pieces + 2
+    keys, values, key_scales, value_scales = pl.pallas_call(
+        functools.partial(hand_on, pieces),
+        out_shape=tuple(jax.ShapeDtypeStruct(a.shape, a.dtype) for a in done),
+        in_specs=[hbm] * 4,
+        out_specs=(hbm,) * 4,
+        scratch_shapes=[pltpu.VMEM(a.shape, a.dtype) for a in done]
+        + [pltpu.SemaphoreType.DMA((moves,)), pltpu.SemaphoreType.DMA((moves,))],
+        compiler_params=pltpu.CompilerParams(vmem_limit_bytes=60 * 1024 * 1024),
+    )(*done)
+    return keys, values, key_scales.T, value_scales.T
 
 
 def solution(mesh):

time: 67.7 us -> 48 us (0.71)
  local copies, waits for them, and re-layouts: 12.5 us -> 0 us
  other arithmetic: 5.29 us -> 0.59 us
  Pallas kernels: 48.6 us -> 46.6 us
    unnamed x4 -> x0, local copies, waits for them, and re-layouts: 6.69 us -> none
    pallas_call x1, Pallas kernels: 48.6 us -> 44.5 us  [shards(): pl.pallas_call(functools.partial(body, n, cap, heads, hd, page), out_shap...]
    pallas_call x2 -> x0, local copies, waits for them, and re-layouts: 2.75 us -> none  [shards(): pl.pallas_call(functools.partial(body, n, cap, heads, hd, page), out_shap...]
    pallas_call x0 -> x1, Pallas kernels: none -> 2.12 us  [shards(): pl.pallas_call(functools.partial(hand_on, pieces), out_shape=tuple((jax.S...]
    reduce_sum x3 -> x0, other arithmetic: 1.46 us -> none  [the longest x1 0.86 us: shards(): src = jnp.sum(jnp.where(hit, lane.reshape(1, -1) + 1, 0), axis=1) - 1]
    concatenate x1 -> x0, other arithmetic: 1.01 us -> none  [shards(): cos_t = jnp.concatenate([cosine, cosine], axis=1)]
    neg x1 -> x0, other arithmetic: 0.99 us -> none  [shards(): sin_t = jnp.concatenate([-sine, sine], axis=1)]
    select_n x1 -> x0, local copies, waits for them, and re-layouts: 0.87 us -> none  [shards(): jnp.where(src[:, None] >= 0, src[:, None] * page + jnp.arange(page)[None,...]
where the time goes in v2:
time: 48 us; the launch traced here: 47.8 us
  Pallas kernels  46.6 us (97%)
  between operations  0.64 us (1%)
  other arithmetic  0.59 us (1%)
    pallas_call x1, Pallas kernels, shards(): pl.pallas_call(functools.partial(body, n, cap, heads, hd, page), out_shap...  44.5 us
    pallas_call x1, Pallas kernels, shards(): pl.pallas_call(functools.partial(hand_on, pieces), out_shape=tuple((jax.S...  2.12 us

profile of v2, /device:TPU:0, one launch (start us, length us, event | category | flops | bytes accessed | tf_op | source)
XLA Modules:
  0.0 47.8 jit_solution(11324335472300998523)
XLA Ops:
  0.6 0.6 %maximum_bitcast_fusion.freq_in = f32[1,128]{1,0:T(1,128)} fusion(f32[64]{0:T(128)S(1)} %multiply_exponential_fusion), kind=kLoop, calls=%fused_computation | loop fusion | flops 128 | bytes 768 | tf_op jit(solution)/shard_map/reshape | solution.py:348
  1.2 44.5 %shard_map.156 = (bf16[79,8,512]{2,1,0:T(8,128)(2,1)}, bf16[79,8,512]{2,1,0:T(8,128)(2,1)}, bf16[4,79]{1,0:T(4,128)(2,1)}, bf16[4,79]{1,0:T(4,128)(2,1)}) custom-call(s32[1,1024]{1,0:T(1,128)} %bitcast.10, s32[1,1024]{1,0:T(1,128)} %bitcast.11, f32[1,128]{1,0:T(1,128)} %maximum_bitcast_fusion.freq_in, f32[1,512]{1,0:T(1,128)} %bitcast.12, ...), custom_call_target="tpu_custom_call" | custom-call | tf_op jit(solution)/shard_map/pallas_call | solution.py:355
  45.7 2.1 %shard_map.157 = (bf16[79,8,512]{2,1,0:T(8,128)(2,1)}, bf16[79,8,512]{2,1,0:T(8,128)(2,1)}, bf16[4,79]{1,0:T(4,128)(2,1)}, bf16[4,79]{1,0:T(4,128)(2,1)}) custom-call(bf16[79,8,512]{2,1,0:T(8,128)(2,1)} %get-tuple-element.12.refs_0_, bf16[79,8,512]{2,1,0:T(8,128)(2,1)} %get-tuple-element.13.refs_1_, bf16[4,79]{1,0:T(4,128)(2,1)} %get-tuple-element.14.refs_2_, ...), custom_call_target="tpu_custom_call" | custom-call | tf_op jit(solution)/shard_map/pallas_call | solution.py:412
  (1 shorter events, 0.0 us)
